TPU v7x, 32 devices: a whole 2x2x4 slice. The times are simulated.
32 devices in a mesh: dp: 8 (over z, x), expert: 4 (over y, core).
Axes of the slice: x: 2, y: 2, z: 4, core: 2. Of those that a mesh axis runs over, the one named last changes fastest.
Arguments:
- tokens: bfloat16 [2048, 2048], P('dp'), may hold values from -6 to 6
- routes: int32 [2048, 6], P('dp'), may hold values from 0 to 63, all different within a row; in each aligned block of 256 rows (0 to 255, 256 to 511, ...) at most 32 rows name the same one
- gates: float32 [2048, 6], P('dp'), may hold values from 0.1 to 1
- w_gate: bfloat16 [64, 2048, 1408], P('dp', None, 'expert'), may hold values from -0.125 to 0.125
- w_up: bfloat16 [64, 2048, 1408], P('dp', None, 'expert'), may hold values from -0.125 to 0.125
- w_down: bfloat16 [64, 1408, 2048], P('dp', 'expert'), may hold values from -0.21875 to 0.21875
- s_gate: bfloat16 [2048, 2816], P(None, 'expert'), may hold values from -0.125 to 0.125
- s_up: bfloat16 [2048, 2816], P(None, 'expert'), may hold values from -0.125 to 0.125
- s_down: bfloat16 [2816, 2048], P('expert'), may hold values from -0.15625 to 0.15625
Outputs:
- mixed: bfloat16 [2048, 2048], P('dp', 'expert')
Inputs may be any that keep to these rules, and one draw needn't show every extreme that they name: `routes`: each row names 6 different experts. Within each aligned block of 256 rows (the rows of one index of dp) no expert is named by more than 32 rows; some expert is named by exactly 32 rows in some block of every draw.
All inputs are finite; a program needn't handle non-finite values.
Results may differ from a plain program's by a relative error of at most 0.013.
Values may be sent and summed in bfloat16 or wider, within the bound.
A program may use at most 128 MiB of HBM per device.

v0:
```python
import jax
import jax.numpy as jnp
from jax import lax
from jax.sharding import PartitionSpec as P

CAP = 32


def body(tokens, routes, gates, w_gate, w_up, w_down, s_gate, s_up, s_down):
    tok_rows, width = tokens.shape
    local_experts = w_gate.shape[0]
    groups = lax.axis_size("dp")
    members = lax.axis_size("expert")
    experts_all = local_experts * groups
    top_count = routes.shape[1]
    capacity = CAP
    quarter = width // members
    labels = jnp.arange(experts_all, dtype=jnp.int32)
    matches = (routes[:, :, None] == labels[None, None, :]).astype(jnp.int32)
    counts = jnp.sum(matches, axis=1)
    before = jnp.cumsum(counts, axis=0) - counts
    slots = jnp.sum(matches * before[:, None, :], axis=2)
    dest = routes * capacity + slots
    token_ids = jnp.repeat(jnp.arange(tok_rows, dtype=jnp.int32), top_count)
    sources = (
        jnp.full((experts_all * capacity,), tok_rows, jnp.int32).at[dest.reshape(-1)].set(token_ids)
    )
    padded = jnp.concatenate([tokens, jnp.zeros((1, width), tokens.dtype)], axis=0)
    outgoing = padded[sources].reshape(groups, local_experts, capacity, width)
    offset = lax.axis_index("expert") * quarter
    outgoing = lax.dynamic_slice_in_dim(outgoing, offset, quarter, 3)
    received = lax.all_to_all(outgoing, "dp", split_axis=0, concat_axis=0, tiled=True)
    received = lax.all_gather(received, "expert", axis=3, tiled=True)
    gate = jnp.einsum("sjcd,jdf->sjcf", received, w_gate, preferred_element_type=jnp.float32)
    up = jnp.einsum("sjcd,jdf->sjcf", received, w_up, preferred_element_type=jnp.float32)
    hidden = (jax.nn.silu(gate) * up).astype(jnp.bfloat16)
    partial_value = jnp.einsum("sjcf,jfd->sjcd", hidden, w_down, preferred_element_type=jnp.float32)
    summed = lax.psum_scatter(
        partial_value.astype(jnp.bfloat16), "expert", scatter_dimension=3, tiled=True
    )
    returned = lax.all_to_all(summed, "dp", split_axis=0, concat_axis=0, tiled=True)
    flat = returned.reshape(experts_all * capacity, quarter)
    picked = flat[dest].astype(jnp.float32)
    routed = jnp.einsum("tk,tkd->td", gates, picked)
    shared_gate = jnp.dot(tokens, s_gate, preferred_element_type=jnp.float32)
    shared_up = jnp.dot(tokens, s_up, preferred_element_type=jnp.float32)
    shared_hidden = (jax.nn.silu(shared_gate) * shared_up).astype(jnp.bfloat16)
    shared_part = jnp.dot(shared_hidden, s_down, preferred_element_type=jnp.float32)
    shared_out = lax.psum_scatter(
        shared_part.astype(jnp.bfloat16), "expert", scatter_dimension=1, tiled=True
    ).astype(jnp.float32)
    return (shared_out + routed).astype(jnp.bfloat16)


def solution(mesh):
    placed = (
        P("dp", None),
        P("dp", None),
        P("dp", None),
        P("dp", None, "expert"),
        P("dp", None, "expert"),
        P("dp", "expert", None),
        P(None, "expert"),
        P(None, "expert"),
        P("expert", None),
    )
    return jax.shard_map(
        body, mesh=mesh, in_specs=placed, out_specs=P("dp", "expert"), check_vma=False
    )
```

profile of v0, /device:TPU:0, one launch (start us, length us, event | category | flops | bytes accessed | tf_op | source)
XLA Modules:
  0.0 341.5 jit_solution(1969258154155409684)
XLA Ops:
  6.5 0.0 copy-start
  6.5 0.0 all-gather.2.cloned.1.call-start
  6.5 0.9 convert_reduce_fusion
  7.5 0.6 reduce-window.6
  8.1 0.2 slice_reduce_fusion
  8.3 0.1 fusion.17
  8.4 0.8 select_reduce_fusion
  9.1 0.7 compare_select_fusion.1
  9.9 0.1 copy.29
  10.0 0.1 reshape.54
  10.2 0.1 reshape.78
  10.3 6.2 %scatter_custom_fusion = s32[2048]{0:T(1024)S(1)} fusion(s32[1536]{0:T(1024)S(1)} %fusion.19, s32[1536]{0:T(1024)S(1)} %reshape.78, s32[]{:T(128)} %constant.11.clone.1), kind=kCustom, calls=%fused_computation.38 | custom fusion | bytes 8196 | tf_op jit(solution)/shard_map/scatter | solution.py:26
  16.5 2.4 concatenate.3
  19.0 17.7 %gather_fusion = bf16[2048,2048]{1,0:T(8,128)(2,1)} fusion(bf16[257,2048]{1,0:T(8,128)(2,1)} %concatenate.3, s32[2048]{0:T(1024)S(1)} %fusion.18), kind=kCustom, calls=%fused_computation | custom fusion | bytes 16785408 | tf_op jit(solution)/shard_map/gather | solution.py:29
  36.7 1.8 constant_dynamic-slice_fusion
  38.5 55.3 %all_to_all.10 = bf16[8,8,32,512]{3,2,1,0:T(8,128)(2,1)S(1)} all-to-all(bf16[8,8,32,512]{3,2,1,0:T(8,128)(2,1)S(1)} %constant_dynamic-slice_fusion), channel_id=1, replica_groups=mesh['dp'=8,'expert'=4] {'dp'}, dimensions={0} | all-to-all | bytes 4194304 | tf_op jit(solution)/shard_map/all_to_all | solution.py:32
  93.8 1.6 copy.30
  95.5 0.0 all-gather.2.cloned.1.call-update
  95.5 0.2 reduce-scatter.5.cloned.1.call-start
  95.7 57.2 %all-gather.2.cloned.1.call-done = bf16[8,8,32,2048]{3,2,0,1:T(8,128)(2,1)} async-done(((bf16[8,8,32,512]{3,2,0,1:T(8,128)(2,1)}), bf16[8,8,32,2048]{3,2,0,1:T(8,128)(2,1)}) %all-gather.2.cloned.1.call-update) | async-done | bytes 8388624 | tf_op jit(solution)/shard_map/all_gather | solution.py:33
  152.9 12.9 %fusion.4 = f32[8,8,32,352]{3,2,1,0:T(8,128)} fusion(bf16[8,8,32,2048]{3,2,0,1:T(8,128)(2,1)} %all-gather.2.cloned.1.call-done, bf16[8,2048,352]{1,2,0:T(8,128)(2,1)} %param.12), kind=kOutput, calls=%fused_computation.7 | convolution fusion | flops 2952790016 | bytes 22806528 | tf_op jit(solution)/shard_map/sjcd,jdf->sjcf/dot_general | solution.py:34
  165.9 13.3 %fusion.8 = bf16[8,8,32,352]{3,2,0,1:T(8,128)(2,1)} fusion(f32[8,8,32,352]{3,2,1,0:T(8,128)} %fusion.4, bf16[8,8,32,2048]{3,2,0,1:T(8,128)(2,1)} %all-gather.2.cloned.1.call-done, bf16[8,2048,352]{1,2,0:T(8,128)(2,1)} %param.13), kind=kOutput, calls=%fused_computation.11 | convolution fusion | flops 2957115392 | bytes 24248320 | tf_op jit(solution)/shard_map/sjcd,jdf->sjcf/dot_general | solution.py:35
  179.1 12.5 %convert_bitcast_fusion = bf16[8,8,32,2048]{3,2,0,1:T(8,128)(2,1)} fusion(bf16[8,8,32,352]{3,2,0,1:T(8,128)(2,1)} %fusion.8, bf16[8,352,2048]{2,1,0:T(8,128)(2,1)} %param.14), kind=kOutput, calls=%fused_computation.9 | convolution fusion | flops 2956984320 | bytes 21364736 | tf_op jit(solution)/shard_map/sjcf,jfd->sjcd/dot_general | solution.py:37
  191.6 0.0 reduce-scatter.5.cloned.1.call-update
  191.7 71.4 %reduce-scatter.5.cloned.1.call-done = bf16[8,8,32,512]{3,2,0,1:T(8,128)(2,1)} async-done(((bf16[8,8,32,2048]{3,2,0,1:T(8,128)(2,1)}), bf16[8,8,32,512]{3,2,0,1:T(8,128)(2,1)}) %reduce-scatter.5.cloned.1.call-update) | async-done | bytes 2097168 | tf_op jit(solution)/shard_map/reduce_scatter | solution.py:38
  263.0 3.1 copy.31
  266.2 5.5 %all-to-all-start.1 = ((bf16[8,8,32,512]{3,2,1,0:T(8,128)(2,1)}), bf16[8,8,32,512]{3,2,1,0:T(8,128)(2,1)}, u32[]{:S(2)}, u32[]{:S(2)}) async-start(bf16[8,8,32,512]{3,2,1,0:T(8,128)(2,1)} %copy.31), calls=%async_computation.3 | async-start | bytes 4194304 | tf_op jit(solution)/shard_map/all_to_all | solution.py:41
  271.7 0.3 reduce-scatter.3.cloned.1.call-start
  272.0 4.0 %fusion.23 = f32[256,704]{0,1:T(8,128)} fusion(bf16[256,2048]{1,0:T(8,128)(2,1)} %param.9, bf16[2048,704]{0,1:T(8,128)(2,1)} %param.15), kind=kOutput, calls=%fused_computation.42 | convolution fusion | flops 738197504 | bytes 4653056 | tf_op jit(solution)/shard_map/dot_general | solution.py:45
  275.9 0.0 copy-done
  275.9 0.0 copy-start.1
  275.9 6.6 %convolution_convert_fusion = bf16[256,2048]{1,0:T(8,128)(2,1)} fusion(bf16[704,2048]{1,0:T(8,128)(2,1)S(1)} %copy-done, bf16[256,2048]{1,0:T(8,128)(2,1)} %param.9, bf16[2048,704]{0,1:T(8,128)(2,1)} %param.16, f32[256,704]{0,1:T(8,128)} %fusion.23), kind=kOutput, calls=%fused_computation.17 | convolution fusion | flops 1478000640 | bytes 8585216 | tf_op jit(solution)/shard_map/dot_general | solution.py:48
  282.5 0.0 reduce-scatter.3.cloned.1.call-update
  282.5 0.1 copy.32
  282.7 0.1 reshape.68
  282.8 0.0 copy-done.1
  282.8 0.2 copy.36
  283.0 36.9 %all-to-all-done.1 = bf16[8,8,32,512]{3,2,1,0:T(8,128)(2,1)} async-done(((bf16[8,8,32,512]{3,2,1,0:T(8,128)(2,1)}), bf16[8,8,32,512]{3,2,1,0:T(8,128)(2,1)}, u32[]{:S(2)}, u32[]{:S(2)}) %all-to-all-start.1) | async-done | bytes 2097184 | tf_op jit(solution)/shard_map/all_to_all | solution.py:41
  319.9 7.4 %gather_fusion.1 = bf16[1536,512]{1,0:T(8,128)(2,1)} fusion(bf16[2048,512]{1,0:T(8,128)(2,1)} %bitcast.12, s32[2048]{0:T(1024)S(1)} %pad_clamp_fusion), kind=kCustom, calls=%fused_computation.1 | custom fusion | bytes 3151872 | tf_op jit(solution)/shard_map/gather | solution.py:43
  327.2 3.7 %reshape.67 = bf16[256,6,512]{2,1,0:T(8,128)(2,1)} reshape(bf16[1536,512]{1,0:T(8,128)(2,1)} %gather_fusion.1) | data formatting | bytes 3145728 | tf_op jit(solution)/shard_map/gather | solution.py:43
  331.0 2.3 fusion.24
  333.2 0.0 reduce-scatter.3.cloned.1.call-done
  333.3 1.7 fusion.15
  (7 shorter events, 0.1 us)
Async XLA Ops:
  6.5 269.4 %copy-start = (bf16[704,2048]{1,0:T(8,128)(2,1)S(1)}, bf16[704,2048]{1,0:T(8,128)(2,1)}, u32[]{:S(2)}) copy-start(bf16[704,2048]{1,0:T(8,128)(2,1)} %param.17) | copy-start | bytes 8650756
  6.5 146.4 %all-gather.2.cloned.1.call-start = ((), (), s32[]{:S(2)}) async-start(), calls=%async_computation.5 | async-start | bytes 10485760 | tf_op jit(solution)/shard_map/all_gather | solution.py:33
  95.5 167.6 %reduce-scatter.5.cloned.1.call-start = ((), (), s32[]{:S(2)}) async-start(), calls=%async_computation.6 | async-start | bytes 10485760 | tf_op jit(solution)/shard_map/reduce_scatter | solution.py:38
  266.2 53.7 %all-to-all-start.1 = ((bf16[8,8,32,512]{3,2,1,0:T(8,128)(2,1)}), bf16[8,8,32,512]{3,2,1,0:T(8,128)(2,1)}, u32[]{:S(2)}, u32[]{:S(2)}) async-start(bf16[8,8,32,512]{3,2,1,0:T(8,128)(2,1)} %copy.31), calls=%async_computation.3 | async-start | bytes 4194304 | tf_op jit(solution)/shard_map/all_to_all | solution.py:41
  271.7 61.6 %reduce-scatter.3.cloned.1.call-start = ((), (), s32[]{:S(2)}) async-start(), calls=%async_computation.4 | async-start | bytes 1310720 | tf_op jit(solution)/shard_map/reduce_scatter | solution.py:49
  275.9 6.9 %copy-start.1 = (f32[256,6]{0,1:T(8,128)S(1)}, f32[256,6]{0,1:T(8,128)}, u32[]{:S(2)}) copy-start(f32[256,6]{0,1:T(8,128)} %param.11) | copy-start | bytes 18436
Sparse Core Ops, SparseCore 0:
  95.6 57.2 all-gather.1
  191.8 71.2 reduce-scatter.4
  282.7 25.0 reduce-scatter.2
where the time goes:
time: 342 us
  waiting for transfers between devices  166 us (49%)
  blocking collectives  55.3 us (16%)
  matrix products  51.5 us (15%)
  local copies, waits for them, and re-layouts  45.1 us (13%)
  between operations  13.3 us (4%)
  starting transfers between devices  5.99 us (2%)
  other arithmetic  4.86 us (1%)
    reduce_scatter x1, waiting for transfers between devices, body(): lax.psum_scatter(partial_value.astype(jnp.bfloat16), 'expert', scatter_di...  71.4 us
    all_gather x1, waiting for transfers between devices, body(): received = lax.all_gather(received, 'expert', axis=3, tiled=True)  57.2 us
    all_to_all x1, blocking collectives, body(): lax.all_to_all(outgoing, 'dp', split_axis=0, concat_axis=0, tiled=True)  55.3 us
    all_to_all x1, waiting for transfers between devices, body(): lax.all_to_all(summed, 'dp', split_axis=0, concat_axis=0, tiled=True)  36.9 us
    gather x1, local copies, waits for them, and re-layouts, body(): outgoing = padded[sources].reshape(groups, local_experts, capacity, width)  17.7 us
    dot_general x1, matrix products, body(): jnp.einsum('sjcd,jdf->sjcf', received, w_up, preferred_element_type=jnp.f...  13.3 us
    dot_general x1, matrix products, body(): jnp.einsum('sjcd,jdf->sjcf', received, w_gate, preferred_element_type=jnp...  12.9 us
    dot_general x1, matrix products, body(): jnp.einsum('sjcf,jfd->sjcd', hidden, w_down, preferred_element_type=jnp.f...  12.5 us
  transfers between devices with their start and end apart: 4, of which 3 were waited for; matrix products, arithmetic and copies ran while one was open for 7% of the time, Pallas kernels for 0%

commit v1 on v0

--- a/solution.py
+++ b/solution.py
@@ -30,7 +30,7 @@
     offset = lax.axis_index("expert") * quarter
     outgoing = lax.dynamic_slice_in_dim(outgoing, offset, quarter, 3)
     received = lax.all_to_all(outgoing, "dp", split_axis=0, concat_axis=0, tiled=True)
-    received = lax.all_gather(received, "expert", axis=3, tiled=True)
+    received = jnp.concatenate(lax.all_gather(received, "expert"), axis=3)
     gate = jnp.einsum("sjcd,jdf->sjcf", received, w_gate, preferred_element_type=jnp.float32)
     up = jnp.einsum("sjcd,jdf->sjcf", received, w_up, preferred_element_type=jnp.float32)
     hidden = (jax.nn.silu(gate) * up).astype(jnp.bfloat16)

time: 342 us -> 366 us (1.070)
  local copies, waits for them, and re-layouts: 45.1 us -> 68.8 us
    reshape x1 -> x3, local copies, waits for them, and re-layouts: 0.01 us -> 25.4 us  [the longest x2 25.4 us: body(): received = jnp.concatenate(lax.all_gather(received, 'expert'), axis=3)]
where the time goes in v1:
time: 366 us; the launch traced here: 365 us
  waiting for transfers between devices  166 us (45%)
  local copies, waits for them, and re-layouts  68.8 us (19%)
  blocking collectives  55.4 us (15%)
  matrix products  51.5 us (14%)
  between operations  13.3 us (4%)
  starting transfers between devices  5.81 us (2%)
  other arithmetic  4.86 us (1%)
    reduce_scatter x1, waiting for transfers between devices, body(): lax.psum_scatter(partial_value.astype(jnp.bfloat16), 'expert', scatter_di...  71.4 us
    all_gather x1, waiting for transfers between devices, body(): received = jnp.concatenate(lax.all_gather(received, 'expert'), axis=3)  57.4 us
    all_to_all x1, blocking collectives, body(): lax.all_to_all(outgoing, 'dp', split_axis=0, concat_axis=0, tiled=True)  55.4 us
    all_to_all x1, waiting for transfers between devices, body(): lax.all_to_all(summed, 'dp', split_axis=0, concat_axis=0, tiled=True)  36.9 us
    reshape x2, local copies, waits for them, and re-layouts, body(): received = jnp.concatenate(lax.all_gather(received, 'expert'), axis=3)  25.4 us
    gather x1, local copies, waits for them, and re-layouts, body(): outgoing = padded[sources].reshape(groups, local_experts, capacity, width)  17.7 us
    dot_general x1, matrix products, body(): jnp.einsum('sjcd,jdf->sjcf', received, w_up, preferred_element_type=jnp.f...  13.3 us
    dot_general x1, matrix products, body(): jnp.einsum('sjcd,jdf->sjcf', received, w_gate, preferred_element_type=jnp...  12.9 us
  transfers between devices with their start and end apart: 4, of which 3 were waited for; matrix products, arithmetic and copies ran while one was open for 7% of the time, Pallas kernels for 0%

profile of v1, /device:TPU:0, one launch (start us, length us, event | category | flops | bytes accessed | tf_op | source)
XLA Modules:
  0.0 365.4 jit_solution(10229589518241858550)
XLA Ops:
  6.5 0.0 copy-start
  6.5 0.0 all-gather.3.cloned.1.call-start
  6.5 0.9 convert_reduce_fusion
  7.5 0.6 reduce-window.6
  8.1 0.2 slice_reduce_fusion
  8.3 0.1 fusion.17
  8.4 0.8 select_reduce_fusion
  9.1 0.7 compare_select_fusion.1
  9.9 0.1 copy.29
  10.0 0.1 reshape.60
  10.2 0.1 reshape.86
  10.3 6.2 %scatter_custom_fusion = s32[2048]{0:T(1024)S(1)} fusion(s32[1536]{0:T(1024)S(1)} %fusion.19, s32[1536]{0:T(1024)S(1)} %reshape.86, s32[]{:T(128)} %constant.11.clone.1), kind=kCustom, calls=%fused_computation.38 | custom fusion | bytes 8196 | tf_op jit(solution)/shard_map/scatter | solution.py:26
  16.5 2.4 concatenate.3
  19.0 17.7 %gather_fusion = bf16[2048,2048]{1,0:T(8,128)(2,1)} fusion(bf16[257,2048]{1,0:T(8,128)(2,1)} %concatenate.3, s32[2048]{0:T(1024)S(1)} %fusion.18), kind=kCustom, calls=%fused_computation | custom fusion | bytes 16785408 | tf_op jit(solution)/shard_map/gather | solution.py:29
  36.7 1.8 constant_dynamic-slice_fusion
  38.5 55.4 %all_to_all.10 = bf16[8,8,32,512]{3,2,1,0:T(8,128)(2,1)} all-to-all(bf16[8,8,32,512]{3,2,1,0:T(8,128)(2,1)S(1)} %constant_dynamic-slice_fusion), channel_id=1, replica_groups=mesh['dp'=8,'expert'=4] {'dp'}, dimensions={0} | all-to-all | bytes 4194304 | tf_op jit(solution)/shard_map/all_to_all | solution.py:32
  93.9 0.0 all-gather.3.cloned.1.call-update
  94.0 0.0 reduce-scatter.5.cloned.1.call-start
  94.0 57.4 %all-gather.3.cloned.1.call-done = bf16[32,8,32,512]{3,2,1,0:T(8,128)(2,1)} async-done(((bf16[8,8,32,512]{3,2,1,0:T(8,128)(2,1)}), bf16[32,8,32,512]{3,2,1,0:T(8,128)(2,1)}) %all-gather.3.cloned.1.call-update) | async-done | bytes 8388624 | tf_op jit(solution)/shard_map/all_gather | solution.py:33
  151.4 11.1 %copy.30 = bf16[8,8,32,4,512]{4,3,2,0,1:T(4,128)(2,1)} copy(bf16[8,8,32,4,512]{4,2,1,0,3:T(8,128)(2,1)} %bitcast.78) | data formatting | bytes 16777216 | tf_op jit(solution)/shard_map/reshape | solution.py:33
  162.5 14.3 %reshape.64 = bf16[8,8,32,2048]{3,2,0,1:T(8,128)(2,1)} reshape(bf16[8,8,32,4,512]{4,3,2,0,1:T(4,128)(2,1)} %copy.30) | data formatting | bytes 16777216 | tf_op jit(solution)/shard_map/reshape | solution.py:33
  176.8 12.9 %fusion.4 = f32[8,8,32,352]{3,2,1,0:T(8,128)} fusion(bf16[8,8,32,2048]{3,2,0,1:T(8,128)(2,1)} %reshape.64, bf16[8,2048,352]{1,2,0:T(8,128)(2,1)} %param.12), kind=kOutput, calls=%fused_computation.7 | convolution fusion | flops 2952790016 | bytes 22806528 | tf_op jit(solution)/shard_map/sjcd,jdf->sjcf/dot_general | solution.py:34
  189.7 13.3 %fusion.8 = bf16[8,8,32,352]{3,2,0,1:T(8,128)(2,1)} fusion(f32[8,8,32,352]{3,2,1,0:T(8,128)} %fusion.4, bf16[8,8,32,2048]{3,2,0,1:T(8,128)(2,1)} %reshape.64, bf16[8,2048,352]{1,2,0:T(8,128)(2,1)} %param.13), kind=kOutput, calls=%fused_computation.11 | convolution fusion | flops 2957115392 | bytes 24248320 | tf_op jit(solution)/shard_map/sjcd,jdf->sjcf/dot_general | solution.py:35
  203.0 12.5 %convert_bitcast_fusion = bf16[8,8,32,2048]{3,2,0,1:T(8,128)(2,1)} fusion(bf16[8,8,32,352]{3,2,0,1:T(8,128)(2,1)} %fusion.8, bf16[8,352,2048]{2,1,0:T(8,128)(2,1)} %param.14), kind=kOutput, calls=%fused_computation.9 | convolution fusion | flops 2956984320 | bytes 21364736 | tf_op jit(solution)/shard_map/sjcf,jfd->sjcd/dot_general | solution.py:37
  215.5 0.0 reduce-scatter.5.cloned.1.call-update
  215.6 71.4 %reduce-scatter.5.cloned.1.call-done = bf16[8,8,32,512]{3,2,0,1:T(8,128)(2,1)} async-done(((bf16[8,8,32,2048]{3,2,0,1:T(8,128)(2,1)}), bf16[8,8,32,512]{3,2,0,1:T(8,128)(2,1)}) %reduce-scatter.5.cloned.1.call-update) | async-done | bytes 2097168 | tf_op jit(solution)/shard_map/reduce_scatter | solution.py:38
  286.9 3.1 copy.31
  290.1 5.5 %all-to-all-start.1 = ((bf16[8,8,32,512]{3,2,1,0:T(8,128)(2,1)}), bf16[8,8,32,512]{3,2,1,0:T(8,128)(2,1)}, u32[]{:S(2)}, u32[]{:S(2)}) async-start(bf16[8,8,32,512]{3,2,1,0:T(8,128)(2,1)} %copy.31), calls=%async_computation.3 | async-start | bytes 4194304 | tf_op jit(solution)/shard_map/all_to_all | solution.py:41
  295.6 0.3 reduce-scatter.3.cloned.1.call-start
  295.8 4.0 %fusion.23 = f32[256,704]{0,1:T(8,128)} fusion(bf16[256,2048]{1,0:T(8,128)(2,1)} %param.9, bf16[2048,704]{0,1:T(8,128)(2,1)} %param.15), kind=kOutput, calls=%fused_computation.42 | convolution fusion | flops 738197504 | bytes 4653056 | tf_op jit(solution)/shard_map/dot_general | solution.py:45
  299.8 0.0 copy-done
  299.8 0.0 copy-start.1
  299.8 6.6 %convolution_convert_fusion = bf16[256,2048]{1,0:T(8,128)(2,1)} fusion(bf16[704,2048]{1,0:T(8,128)(2,1)S(1)} %copy-done, bf16[256,2048]{1,0:T(8,128)(2,1)} %param.9, bf16[2048,704]{0,1:T(8,128)(2,1)} %param.16, f32[256,704]{0,1:T(8,128)} %fusion.23), kind=kOutput, calls=%fused_computation.17 | convolution fusion | flops 1478000640 | bytes 8585216 | tf_op jit(solution)/shard_map/dot_general | solution.py:48
  306.4 0.0 reduce-scatter.3.cloned.1.call-update
  306.4 0.1 copy.32
  306.6 0.1 reshape.76
  306.7 0.0 copy-done.1
  306.7 0.2 copy.36
  306.9 36.9 %all-to-all-done.1 = bf16[8,8,32,512]{3,2,1,0:T(8,128)(2,1)} async-done(((bf16[8,8,32,512]{3,2,1,0:T(8,128)(2,1)}), bf16[8,8,32,512]{3,2,1,0:T(8,128)(2,1)}, u32[]{:S(2)}, u32[]{:S(2)}) %all-to-all-start.1) | async-done | bytes 2097184 | tf_op jit(solution)/shard_map/all_to_all | solution.py:41
  343.8 7.4 %gather_fusion.1 = bf16[1536,512]{1,0:T(8,128)(2,1)} fusion(bf16[2048,512]{1,0:T(8,128)(2,1)} %bitcast.14, s32[2048]{0:T(1024)S(1)} %pad_clamp_fusion), kind=kCustom, calls=%fused_computation.1 | custom fusion | bytes 3151872 | tf_op jit(solution)/shard_map/gather | solution.py:43
  351.1 3.7 %reshape.75 = bf16[256,6,512]{2,1,0:T(8,128)(2,1)} reshape(bf16[1536,512]{1,0:T(8,128)(2,1)} %gather_fusion.1) | data formatting | bytes 3145728 | tf_op jit(solution)/shard_map/gather | solution.py:43
  354.9 2.3 fusion.24
  357.1 0.0 reduce-scatter.3.cloned.1.call-done
  357.2 1.7 fusion.15
  (7 shorter events, 0.1 us)
Async XLA Ops:
  6.5 293.3 %copy-start = (bf16[704,2048]{1,0:T(8,128)(2,1)S(1)}, bf16[704,2048]{1,0:T(8,128)(2,1)}, u32[]{:S(2)}) copy-start(bf16[704,2048]{1,0:T(8,128)(2,1)} %param.17) | copy-start | bytes 8650756
  6.5 144.9 %all-gather.3.cloned.1.call-start = ((), (), s32[]{:S(2)}) async-start(), calls=%async_computation.6 | async-start | bytes 10485760 | tf_op jit(solution)/shard_map/all_gather | solution.py:33
  94.0 193.0 %reduce-scatter.5.cloned.1.call-start = ((), (), s32[]{:S(2)}) async-start(), calls=%async_computation.5 | async-start | bytes 10485760 | tf_op jit(solution)/shard_map/reduce_scatter | solution.py:38
  290.1 53.7 %all-to-all-start.1 = ((bf16[8,8,32,512]{3,2,1,0:T(8,128)(2,1)}), bf16[8,8,32,512]{3,2,1,0:T(8,128)(2,1)}, u32[]{:S(2)}, u32[]{:S(2)}) async-start(bf16[8,8,32,512]{3,2,1,0:T(8,128)(2,1)} %copy.31), calls=%async_computation.3 | async-start | bytes 4194304 | tf_op jit(solution)/shard_map/all_to_all | solution.py:41
  295.6 61.6 %reduce-scatter.3.cloned.1.call-start = ((), (), s32[]{:S(2)}) async-start(), calls=%async_computation.4 | async-start | bytes 1310720 | tf_op jit(solution)/shard_map/reduce_scatter | solution.py:49
  299.8 6.9 %copy-start.1 = (f32[256,6]{0,1:T(8,128)S(1)}, f32[256,6]{0,1:T(8,128)}, u32[]{:S(2)}) copy-start(f32[256,6]{0,1:T(8,128)} %param.11) | copy-start | bytes 18436
Sparse Core Ops, SparseCore 0:
  94.1 57.2 all-gather.2
  215.7 71.2 reduce-scatter.4
  306.6 25.0 reduce-scatter.2
